TPU v7x, 32 devices: a whole 2x2x4 slice. The times are simulated.
32 devices in a mesh: dp: 8 (over z, core), tp: 4 (over y, x).
Axes of the slice: x: 2, y: 2, z: 4, core: 2. Of those that a mesh axis runs over, the one named last changes fastest.
Arguments:
- hidden: bfloat16 [384, 4096], P('dp'), may hold values from -6 to 6
- w_qkv: bfloat16 [4096, 4608], P('dp', 'tp'), may hold values from -0.09375 to 0.09375
- w_out: bfloat16 [4096, 4096], P('tp', 'dp'), may hold values from -0.125 to 0.125
- norm_gain: float32 [4096], replicated, may hold values from 0.5 to 1.5
- kv_cache: bfloat16 [384, 2, 128, 256], P(('dp', 'tp')), may hold values from -110 to 110
- lengths: int32 [384], P(('dp', 'tp')), may hold values from 1 to 127, as said below
Outputs:
- residual_out: bfloat16 [384, 4096], P('dp', 'tp')
- scaled: bfloat16 [384, 4096], P('dp', 'tp')
- row_scale: float32 [384], P('dp')
Inputs may be any that keep to these rules, and one draw needn't show every extreme that they name: `lengths`: every sequence has 1 to 127 live positions; among each device's 12 sequences one has exactly 127.
All inputs are finite; a program needn't handle non-finite values.
Results may differ from a plain program's by a relative error of at most 0.015.
Values may be sent and summed in bfloat16 or wider, within the bound.
A program may use at most 64 MiB of HBM per device.

v0:
```python
import jax
import jax.numpy as jnp
from jax import lax
from jax.sharding import PartitionSpec as P


def rope(values, positions):
    half = values.shape[-1] // 2
    freqs = 1000000.0 ** (-2.0 * jnp.arange(half, dtype=jnp.float32) / values.shape[-1])
    angle = positions[..., None] * freqs
    cosine = jnp.cos(angle)
    sine = jnp.sin(angle)
    first = values[..., :half]
    second = values[..., half:]
    return jnp.concatenate(
        [first * cosine - second * sine, second * cosine + first * sine], axis=-1
    )


def shards(hidden, w_qkv, w_out, norm_gain, kv_cache, lengths):
    seq_dev = kv_cache.shape[0]
    kv_heads = kv_cache.shape[1]
    head_size = kv_cache.shape[3] // 2
    tp_count = lax.axis_size("tp")
    w_cols = lax.all_gather(w_qkv, "dp", axis=0, tiled=True)
    qkv_part = jnp.dot(hidden, w_cols, preferred_element_type=jnp.float32)
    mine = lax.all_to_all(
        qkv_part.astype(jnp.bfloat16), "tp", split_axis=0, concat_axis=1, tiled=True
    )
    att_width = w_out.shape[0] * tp_count
    heads = att_width // head_size
    groups = heads // kv_heads
    positions = lengths.astype(jnp.float32)[:, None]
    query = rope(
        mine[:, :att_width].reshape(seq_dev, heads, head_size).astype(jnp.float32), positions
    ).astype(jnp.bfloat16)
    key_new = rope(
        mine[:, att_width : att_width + kv_heads * head_size]
        .reshape(seq_dev, kv_heads, head_size)
        .astype(jnp.float32),
        positions,
    ).astype(jnp.bfloat16)
    value_new = mine[:, att_width + kv_heads * head_size :].reshape(seq_dev, kv_heads, head_size)
    q_grp = query.reshape(seq_dev, kv_heads, groups, head_size)
    keys = kv_cache[..., :head_size]
    vals = kv_cache[..., head_size:]
    scale = 1.0 / head_size**0.5
    scores = jnp.einsum("nkgd,nkpd->nkgp", q_grp, keys, preferred_element_type=jnp.float32) * scale
    own = jnp.einsum("nkgd,nkd->nkg", q_grp, key_new, preferred_element_type=jnp.float32) * scale
    valid = (jnp.arange(kv_cache.shape[2])[None, :] < lengths[:, None])[:, None, None, :]
    scores = jnp.where(valid, scores, jnp.float32(-1e30))
    top = jnp.maximum(jnp.max(scores, axis=-1), own)
    probs = jnp.where(valid, jnp.exp(scores - top[..., None]), jnp.float32(0.0))
    own_prob = jnp.exp(own - top)
    denom = jnp.sum(probs, axis=-1) + own_prob
    weights = (probs / denom[..., None]).astype(jnp.bfloat16)
    own_weight = (own_prob / denom).astype(jnp.bfloat16)
    mixed = jnp.einsum("nkgp,nkpd->nkgd", weights, vals, preferred_element_type=jnp.float32)
    mixed = (
        mixed
        + own_weight.astype(jnp.float32)[..., None] * value_new.astype(jnp.float32)[:, :, None, :]
    )
    attn = mixed.reshape(seq_dev, att_width).astype(jnp.bfloat16)
    heads_part = lax.all_to_all(attn, "tp", split_axis=1, concat_axis=0, tiled=True)
    terms = jnp.dot(
        heads_part,
        lax.all_gather(w_out, "dp", axis=1, tiled=True),
        preferred_element_type=jnp.float32,
    )
    width = terms.shape[1]
    share = width // tp_count
    offset = lax.axis_index("tp") * share
    summed = lax.psum_scatter(
        terms.astype(jnp.bfloat16), "tp", scatter_dimension=1, tiled=True
    ).astype(jnp.float32)
    hidden_mine = lax.dynamic_slice_in_dim(hidden, offset, share, 1).astype(jnp.float32)
    gain_mine = lax.dynamic_slice_in_dim(norm_gain, offset, share, 0)
    resid_mine = hidden_mine + summed
    weighted = resid_mine * gain_mine[None, :]
    squares = lax.psum(jnp.sum(resid_mine * resid_mine, axis=-1), "tp")
    peak = lax.pmax(jnp.max(jnp.abs(weighted), axis=-1), "tp")
    inverse = lax.rsqrt(squares / width + 1e-06)
    normed_mine = weighted * inverse[:, None]
    row_scale = (peak * inverse + 1e-06) / 448.0
    residual_out = resid_mine.astype(jnp.bfloat16)
    scaled = (normed_mine / row_scale[:, None]).astype(jnp.bfloat16)
    return (residual_out, scaled, row_scale)


def solution(mesh):
    placed = (
        P("dp", None),
        P("dp", "tp"),
        P("tp", "dp"),
        P(),
        P(("dp", "tp"), None, None, None),
        P(("dp", "tp")),
    )
    return jax.shard_map(
        shards,
        mesh=mesh,
        in_specs=placed,
        out_specs=(P("dp", "tp"), P("dp", "tp"), P("dp")),
        check_vma=False,
    )
```

profile of v0, /device:TPU:0, one launch (start us, length us, event | category | flops | bytes accessed | tf_op | source)
XLA Modules:
  0.0 241.3 jit_solution(18042979968966744617)
XLA Ops:
  7.2 0.0 all-gather.3.cloned.1.call-start
  7.2 0.7 all-gather.3.cloned.1.call-update
  7.9 0.0 all-gather.5.cloned.1.call-start
  7.9 0.7 all-gather.5.cloned.1.call-update
  8.6 0.7 convert_element_type.66
  9.3 0.1 multiply_cosine_fusion
  9.4 0.0 copy-start.3
  9.5 0.0 copy-start.1
  9.5 93.6 %all-gather.3.cloned.1.call-done = bf16[4096,1152]{1,0:T(8,128)(2,1)} async-done(((bf16[512,1152]{1,0:T(8,128)(2,1)}), bf16[4096,1152]{1,0:T(8,128)(2,1)}) %all-gather.3.cloned.1.call-update) | async-done | bytes 9437200 | tf_op jit(solution)/shard_map/all_gather | solution.py:25
  103.1 5.5 %convolution_convert_fusion.1 = bf16[48,1152]{1,0:T(8,128)(2,1)S(1)} fusion(bf16[48,4096]{1,0:T(8,128)(2,1)} %param.6, bf16[4096,1152]{1,0:T(8,128)(2,1)} %all-gather.3.cloned.1.call-done), kind=kOutput, calls=%fused_computation.1 | convolution fusion | flops 453040128 | bytes 9940992 | tf_op jit(solution)/shard_map/dot_general | solution.py:26
  108.5 0.7 all_to_all.26
  109.2 3.6 %all-to-all-start = ((bf16[4,12,1152]{2,1,0:T(8,128)(2,1)}), bf16[4,12,1152]{2,1,0:T(8,128)(2,1)S(1)}, u32[]{:S(2)}, u32[]{:S(2)}) async-start(bf16[4,12,1152]{2,1,0:T(8,128)(2,1)} %all_to_all.26), calls=%async_computation | async-start | bytes 294912 | tf_op jit(solution)/shard_map/all_to_all | solution.py:27
  112.9 0.0 reduce-scatter.2.cloned.1.call-start
  112.9 0.0 copy-done.3
  112.9 0.1 iota_compare_fusion
  113.0 5.0 %all-to-all-done = bf16[4,12,1152]{2,1,0:T(8,128)(2,1)S(1)} async-done(((bf16[4,12,1152]{2,1,0:T(8,128)(2,1)}), bf16[4,12,1152]{2,1,0:T(8,128)(2,1)S(1)}, u32[]{:S(2)}, u32[]{:S(2)}) %all-to-all-start) | async-done | bytes 110624 | tf_op jit(solution)/shard_map/all_to_all | solution.py:27
  118.0 0.1 pad.4
  118.1 0.1 copy.14
  118.2 0.1 subtract_convert_fusion.1
  118.3 0.1 maximum_bitcast_fusion
  118.4 0.1 subtract_convert_fusion
  118.5 0.2 fusion.10
  118.8 0.0 copy-done.1
  118.8 0.6 fusion.17
  119.5 0.3 fusion.4
  119.8 0.4 fusion.1
  120.1 0.0 copy-start
  120.2 7.5 %all_to_all.35 = bf16[12,4,1024]{2,0,1:T(8,128)(2,1)S(1)} all-to-all(bf16[12,4,1024]{2,0,1:T(8,128)(2,1)S(1)} %copy.10), channel_id=1, replica_groups=mesh['dp'=8,'tp'=4] {'tp'}, dimensions={1} | all-to-all | bytes 196608 | tf_op jit(solution)/shard_map/all_to_all | solution.py:64
  127.8 57.4 %all-gather.5.cloned.1.call-done = bf16[1024,4096]{1,0:T(8,128)(2,1)} async-done(((bf16[1024,512]{1,0:T(8,128)(2,1)}), bf16[1024,4096]{1,0:T(8,128)(2,1)}) %all-gather.5.cloned.1.call-update) | async-done | bytes 8388624 | tf_op jit(solution)/shard_map/all_gather | solution.py:67
  185.2 5.7 %convolution_convert_fusion = bf16[48,4096]{1,0:T(8,128)(2,1)} fusion(bf16[48,1024]{1,0:T(8,128)(2,1)S(1)} %all_to_all.32, bf16[1024,4096]{1,0:T(8,128)(2,1)} %all-gather.5.cloned.1.call-done), kind=kOutput, calls=%fused_computation | convolution fusion | flops 402849792 | bytes 8880128 | tf_op jit(solution)/shard_map/dot_general | solution.py:65
  190.9 0.0 reduce-scatter.2.cloned.1.call-update
  190.9 0.7 dynamic_slice.7
  191.6 22.7 %reduce-scatter.2.cloned.1.call-done = bf16[48,1024]{1,0:T(8,128)(2,1)} async-done(((bf16[48,4096]{1,0:T(8,128)(2,1)}), bf16[48,1024]{1,0:T(8,128)(2,1)}) %reduce-scatter.2.cloned.1.call-update) | async-done | bytes 98320 | tf_op jit(solution)/shard_map/reduce_scatter | solution.py:73
  214.2 0.0 copy-done
  214.3 1.0 multiply_reduce_fusion
  215.3 8.9 %pmax.7 = f32[48]{0:T(128)S(1)} all-reduce(f32[48]{0:T(128)S(1)} %get-tuple-element.4), channel_id=1, replica_groups=mesh['dp'=8,'tp'=4] {'tp'}, use_global_device_ids=true, to_apply=%region_6.7 | all-reduce | flops 48 | bytes 384 | tf_op jit(solution)/shard_map/pmax | solution.py:81
  224.2 8.9 %psum.7 = f32[48]{0:T(128)S(1)} all-reduce(f32[48]{0:T(128)S(1)} %get-tuple-element.3), channel_id=1, replica_groups=mesh['dp'=8,'tp'=4] {'tp'}, use_global_device_ids=true, to_apply=%region_4.5 | all-reduce | flops 48 | bytes 384 | tf_op jit(solution)/shard_map/psum | solution.py:80
  233.1 0.0 copy-start.2
  233.1 1.6 divide_convert_fusion
  234.8 0.0 copy-done.2
  (14 shorter events, 0.3 us)
Async XLA Ops:
  7.2 95.9 %all-gather.3.cloned.1.call-start = ((), (), s32[]{:S(2)}) async-start(), calls=%async_computation.3 | async-start | bytes 10616832 | tf_op jit(solution)/shard_map/all_gather | solution.py:25
  7.9 177.3 %all-gather.5.cloned.1.call-start = ((), (), s32[]{:S(2)}) async-start(), calls=%async_computation.4 | async-start | bytes 9437184 | tf_op jit(solution)/shard_map/all_gather | solution.py:67
  9.4 103.4 %copy-start.3 = (s32[12]{0:T(128)S(1)}, s32[12]{0:T(128)}, u32[]{:S(2)}) copy-start(s32[12]{0:T(128)} %param.11) | copy-start | bytes 148
  9.5 109.3 %copy-start.1 = (bf16[12,2,128,256]{3,2,1,0:T(8,128)(2,1)S(1)}, bf16[12,2,128,256]{3,2,1,0:T(8,128)(2,1)}, u32[]{:S(2)}) copy-start(bf16[12,2,128,256]{3,2,1,0:T(8,128)(2,1)} %param.10) | copy-start | bytes 4718596
  109.2 8.7 %all-to-all-start = ((bf16[4,12,1152]{2,1,0:T(8,128)(2,1)}), bf16[4,12,1152]{2,1,0:T(8,128)(2,1)S(1)}, u32[]{:S(2)}, u32[]{:S(2)}) async-start(bf16[4,12,1152]{2,1,0:T(8,128)(2,1)} %all_to_all.26), calls=%async_computation | async-start | bytes 294912 | tf_op jit(solution)/shard_map/all_to_all | solution.py:27
  112.9 101.4 %reduce-scatter.2.cloned.1.call-start = ((), (), s32[]{:S(2)}) async-start(), calls=%async_computation.5 | async-start | bytes 491520 | tf_op jit(solution)/shard_map/reduce_scatter | solution.py:73
  120.1 94.1 %copy-start = (bf16[48,4096]{1,0:T(8,128)(2,1)S(1)}, bf16[48,4096]{1,0:T(8,128)(2,1)}, u32[]{:S(2)}) copy-start(bf16[48,4096]{1,0:T(8,128)(2,1)} %param.6) | copy-start | bytes 1179652
  233.1 1.6 copy-start.2
Sparse Core Ops, SparseCore 0:
  9.6 93.4 all-gather.2
  104.7 80.4 all-gather.4
  191.0 23.1 reduce-scatter.1
where the time goes:
time: 242 us; the launch traced here: 241 us
  waiting for transfers between devices  180 us (74%)
  blocking collectives  25.3 us (10%)
  between operations  13.9 us (6%)
  matrix products  12.4 us (5%)
  other arithmetic  4.18 us (2%)
  starting transfers between devices  3.72 us (2%)
    all_gather x1, waiting for transfers between devices, shards(): w_cols = lax.all_gather(w_qkv, 'dp', axis=0, tiled=True)  93.6 us
    all_gather x1, waiting for transfers between devices, shards(): lax.all_gather(w_out, 'dp', axis=1, tiled=True)  57.4 us
    reduce_scatter x1, waiting for transfers between devices, shards(): lax.psum_scatter(terms.astype(jnp.bfloat16), 'tp', scatter_dimension=1, t...  22.7 us
    pmax x1, blocking collectives, shards(): peak = lax.pmax(jnp.max(jnp.abs(weighted), axis=-1), 'tp')  8.93 us
    psum x1, blocking collectives, shards(): squares = lax.psum(jnp.sum(resid_mine * resid_mine, axis=-1), 'tp')  8.87 us
    all_to_all x1, blocking collectives, shards(): lax.all_to_all(attn, 'tp', split_axis=1, concat_axis=0, tiled=True)  7.54 us
    dot_general x1, matrix products, shards(): jnp.dot(heads_part, lax.all_gather(w_out, 'dp', axis=1, tiled=True), pref...  5.7 us
    dot_general x1, matrix products, shards(): qkv_part = jnp.dot(hidden, w_cols, preferred_element_type=jnp.float32)  5.46 us
  transfers between devices with their start and end apart: 4, of which 4 were waited for; matrix products, arithmetic and copies ran while one was open for 4% of the time, Pallas kernels for 0%

commit v1 on v0

--- a/solution.py
+++ b/solution.py
@@ -1,6 +1,10 @@
+import functools
+
 import jax
 import jax.numpy as jnp
 from jax import lax
+from jax.experimental import pallas as pl
+from jax.experimental.pallas import tpu as pltpu
 from jax.sharding import PartitionSpec as P
 
 
@@ -87,6 +91,331 @@
     return (residual_out, scaled, row_scale)
 
 
+F32 = jnp.float32
+BF16 = jnp.bfloat16
+MESH = pl.DeviceIdType.MESH
+
+
+def send(src, dst, send_sem, recv_sem, where):
+    copy = pltpu.make_async_remote_copy(
+        src_ref=src, dst_ref=dst, send_sem=send_sem, recv_sem=recv_sem,
+        device_id=where, device_id_type=MESH,
+    )
+    copy.start()
+    return copy
+
+
+def layer(
+    n_dp, n_tp,
+    hidden, w_qkv, w_out, gain, cache, lens,
+    resid_out, scaled_out, scale_out,
+    h_all, w1, w2, kv, hid, hid32, p_send, p_recv, r_acc, r_send, r_recv, mine32,
+    t1_send, t1_recv, q_rows, k_rows, v_rows, l_rows, s_rows, a_rows,
+    t2_send, t2_recv, b_rows, ag, mm, mq, t3_send, t3_recv, f_send, f_recv,
+    o_send, o_recv, c_send, c_recv, fin,
+    loc_sem, h_s, h_r, p_s, p_r, r_s, r_r, t1_s, t1_r, t2_s, t2_r,
+    g_s, g_r, x_s, t3_s, t3_r, f_s, f_r, o_s, o_r, c_s, c_r,
+):
+    dp = lax.axis_index("dp")
+    tp = lax.axis_index("tp")
+    core = lax.rem(dp, 2)
+    chip = dp // 2
+    other = 1 - core
+    partner = chip * 2 + other
+    n_chip = n_dp // 2
+    rows = hidden.shape[0]
+    seqs = rows // n_tp
+    depth = w_qkv.shape[0]
+    ocols = w_out.shape[1]
+    owide = resid_out.shape[1]
+    kvh = cache.shape[1]
+    ctx = cache.shape[2]
+    hd = cache.shape[3] // 2
+    heads = (w_out.shape[0] * n_tp) // hd
+    groups = heads // kvh
+    per = w_qkv.shape[1] // hd
+    per_out = w_out.shape[0] // hd
+    width = hidden.shape[1]
+
+    own_h = pltpu.make_async_copy(
+        hidden.at[:, pl.ds(pl.multiple_of(dp * depth, depth), depth)], h_all.at[core, chip], loc_sem.at[0])
+    own_h.start()
+    load_w1 = pltpu.make_async_copy(w_qkv, w1, loc_sem.at[1])
+    load_w1.start()
+
+    barrier = pltpu.get_barrier_semaphore()
+    for d in range(1, n_dp):
+        pl.semaphore_signal(barrier, inc=1, device_id={"dp": lax.rem(dp + d, n_dp)}, device_id_type=MESH)
+    for d in range(1, n_tp):
+        pl.semaphore_signal(barrier, inc=1, device_id={"tp": lax.rem(tp + d, n_tp)}, device_id_type=MESH)
+    pl.semaphore_wait(barrier, n_dp + n_tp - 2)
+
+    pending = []
+    for d in range(1, n_dp):
+        peer = lax.rem(dp + d, n_dp)
+        pending.append(send(
+            hidden.at[:, pl.ds(pl.multiple_of(peer * depth, depth), depth)],
+            h_all.at[core, chip], h_s.at[peer], h_r.at[dp], {"dp": peer}))
+    load_kv = pltpu.make_async_copy(cache, kv, loc_sem.at[2])
+    load_kv.start()
+    load_w2 = pltpu.make_async_copy(w_out, w2, loc_sem.at[3])
+    load_w2.start()
+    load_hid = pltpu.make_async_copy(hidden, hid, loc_sem.at[4])
+    load_hid.start()
+
+    row_i = lax.broadcasted_iota(jnp.int32, (seqs, hd), 0)
+    lane_i = lax.broadcasted_iota(jnp.int32, (seqs, hd), 1)
+    live = jnp.zeros((seqs, hd), jnp.int32)
+    for n in range(seqs):
+        live = jnp.where(row_i == n, lens[n], live)
+    half = hd // 2
+    low = lane_i < half
+    index = jnp.where(low, lane_i, lane_i - half).astype(F32)
+    freqs = jnp.exp(index * F32(-2.0 * 13.815510557964274 / hd))
+    angle = live.astype(F32) * freqs
+    cosine = jnp.cos(angle)
+    sine = jnp.where(low, -jnp.sin(angle), jnp.sin(angle))
+    for h in range(heads):
+        l_rows[pl.ds(h, seqs, stride=heads), :] = live.astype(F32)
+    load_hid.wait()
+    hid32[...] = hid[...].astype(F32)
+
+    def recv_h(peer):
+        pltpu.make_async_remote_copy(
+            src_ref=h_all.at[core, chip], dst_ref=h_all.at[lax.rem(peer, 2), peer // 2],
+            send_sem=h_s.at[peer], recv_sem=h_r.at[peer],
+            device_id={"dp": peer}, device_id_type=MESH).wait_recv()
+
+    own_h.wait()
+    load_w1.wait()
+    for d in range(n_chip):
+        recv_h(2 * d + other)
+    part = jnp.dot(h_all[other].reshape(n_chip * rows, depth), w1[...], preferred_element_type=F32)
+    p_send[...] = part.astype(BF16).reshape(p_send.shape)
+    swap = send(p_send, p_recv, p_s, p_r, {"dp": partner})
+    pending.append(swap)
+    for d in range(1, n_chip):
+        recv_h(2 * lax.rem(chip + d, n_chip) + core)
+    part = jnp.dot(h_all[core].reshape(n_chip * rows, depth), w1[...], preferred_element_type=F32)
+    r_acc[...] = part.reshape(r_acc.shape)
+    swap.wait_recv()
+    for d in range(1, n_chip):
+        to = lax.rem(chip + d, n_chip)
+        r_send[to] = (r_acc[to] + p_recv[to].astype(F32)).astype(BF16)
+        pending.append(send(r_send.at[to], r_recv.at[chip], r_s.at[to], r_r.at[chip], {"dp": to * 2 + core}))
+    total = r_acc[chip] + p_recv[chip].astype(F32)
+    for d in range(1, n_chip):
+        who = lax.rem(chip + d, n_chip)
+        pltpu.make_async_remote_copy(
+            src_ref=r_send.at[who], dst_ref=r_recv.at[who], send_sem=r_s.at[who], recv_sem=r_r.at[who],
+            device_id={"dp": who * 2 + core}, device_id_type=MESH).wait_recv()
+        total = total + r_recv[who].astype(F32)
+    mine32[...] = total
+
+    def exchange(src, dst, s_sem, r_sem, fill):
+        for q in range(n_tp):
+            fill(q)
+        keep = pltpu.make_async_copy(src.at[tp], dst.at[tp], r_sem.at[tp])
+        keep.start()
+        sent = []
+        for d in range(1, n_tp):
+            peer = lax.rem(tp + d, n_tp)
+            sent.append(send(src.at[peer], dst.at[tp], s_sem.at[peer], r_sem.at[tp], {"tp": peer}))
+        keep.wait()
+        for d in range(1, n_tp):
+            peer = lax.rem(tp + d, n_tp)
+            pltpu.make_async_remote_copy(
+                src_ref=src.at[peer], dst_ref=dst.at[peer], send_sem=s_sem.at[peer], recv_sem=r_sem.at[peer],
+                device_id={"tp": peer}, device_id_type=MESH).wait_recv()
+        return sent
+
+    def fill1(q):
+        t1_send[q] = mine32[q * seqs : (q + 1) * seqs, :].astype(BF16)
+
+    pending += exchange(t1_send, t1_recv, t1_s, t1_r, fill1)
+
+    def head(h):
+        return t1_recv[h // per, :, (h % per) * hd : (h % per + 1) * hd].astype(F32)
+
+    def turn(x):
+        return (x * cosine + pltpu.roll(x, half, 1) * sine).astype(BF16).astype(F32)
+
+    for h in range(heads):
+        q_rows[pl.ds(h, seqs, stride=heads), :] = turn(head(h))
+    for k in range(kvh):
+        key_new = turn(head(heads + k))
+        value_new = head(heads + kvh + k)
+        for g in range(groups):
+            k_rows[pl.ds(k * groups + g, seqs, stride=heads), :] = key_new
+            v_rows[pl.ds(k * groups + g, seqs, stride=heads), :] = value_new
+    load_kv.wait()
+    for n in range(seqs):
+        for k in range(kvh):
+            at = (n * kvh + k) * groups
+            s_rows[at : at + groups, :] = lax.dot_general(
+                q_rows[at : at + groups, :].astype(BF16), kv[n, k, :, :hd],
+                (((1,), (1,)), ((), ())), preferred_element_type=F32)
+    factor = F32(1.0 / hd**0.5)
+    pos = lax.broadcasted_iota(jnp.int32, (seqs * heads, ctx), 1).astype(F32)
+    valid = pos < l_rows[...]
+    scores = jnp.where(valid, s_rows[...] * factor, F32(-1e30))
+    own = jnp.sum(q_rows[...] * k_rows[...], axis=1, keepdims=True) * factor
+    top = jnp.maximum(jnp.max(scores, axis=1, keepdims=True), own)
+    probs = jnp.where(valid, jnp.exp(scores - top), F32(0.0))
+    own_prob = jnp.exp(own - top)
+    denom = jnp.sum(probs, axis=1, keepdims=True) + own_prob
+    s_rows[...] = probs / denom
+    own_weight = (own_prob / denom).astype(BF16).astype(F32)
+    v_rows[...] = own_weight * v_rows[...]
+    for n in range(seqs):
+        for k in range(kvh):
+            at = (n * kvh + k) * groups
+            a_rows[at : at + groups, :] = jnp.dot(
+                s_rows[at : at + groups, :].astype(BF16), kv[n, k, :, hd:],
+                preferred_element_type=F32) + v_rows[at : at + groups, :]
+
+    def fill2(q):
+        for e in range(per_out):
+            t2_send[q, :, e * hd : (e + 1) * hd] = a_rows[
+                pl.ds(q * per_out + e, seqs, stride=heads), :].astype(BF16)
+
+    pending += exchange(t2_send, t2_recv, t2_s, t2_r, fill2)
+    for q in range(n_tp):
+        b_rows[q * seqs : (q + 1) * seqs, :] = t2_recv[q].astype(F32)
+    ag[core, chip] = b_rows[...].astype(BF16)
+    for d in range(1, n_chip):
+        to = lax.rem(chip + d, n_chip)
+        pending.append(send(ag.at[core, chip], ag.at[core, chip], g_s.at[to], g_r.at[core, chip],
+                            {"dp": to * 2 + core}))
+    pending.append(send(ag.at[core, chip], ag.at[core, chip], x_s.at[chip], g_r.at[core, chip], {"dp": partner}))
+
+    def recv_g(c, who):
+        pltpu.make_async_remote_copy(
+            src_ref=ag.at[core, chip], dst_ref=ag.at[c, who], send_sem=x_s.at[chip], recv_sem=g_r.at[c, who],
+            device_id={"dp": partner}, device_id_type=MESH).wait_recv()
+
+    for d in range(1, n_chip):
+        who = lax.rem(chip + d, n_chip)
+        recv_g(core, who)
+        pending.append(send(ag.at[core, who], ag.at[core, who], x_s.at[who], g_r.at[core, who], {"dp": partner}))
+    load_w2.wait()
+    mm[core] = jnp.dot(ag[core].reshape(n_chip * rows, w_out.shape[0]), w2[...],
+                       preferred_element_type=F32).reshape(n_chip, rows, ocols)
+    for d in range(n_chip):
+        recv_g(other, d)
+    mm[other] = jnp.dot(ag[other].reshape(n_chip * rows, w_out.shape[0]), w2[...],
+                        preferred_element_type=F32).reshape(n_chip, rows, ocols)
+
+    def fill3(q):
+        for r in range(n_dp):
+            mq[q, r * seqs : (r + 1) * seqs, :] = mm[r % 2, r // 2, q * seqs : (q + 1) * seqs, :]
+        t3_send[q] = mq[q].astype(BF16)
+
+    pending += exchange(t3_send, t3_recv, t3_s, t3_r, fill3)
+    total = t3_recv[0].astype(F32)
+    for q in range(1, n_tp):
+        total = total + t3_recv[q].astype(F32)
+    mq[0] = total
+    for r in range(n_dp):
+        f_send[r] = mq[0, r * seqs : (r + 1) * seqs, :].astype(BF16)
+    keep = pltpu.make_async_copy(f_send.at[dp], f_recv.at[dp], f_r.at[dp])
+    keep.start()
+    for d in range(1, n_dp):
+        peer = lax.rem(dp + d, n_dp)
+        pending.append(send(f_send.at[peer], f_recv.at[dp], f_s.at[peer], f_r.at[dp], {"dp": peer}))
+    keep.wait()
+    for d in range(1, n_dp):
+        peer = lax.rem(dp + d, n_dp)
+        pltpu.make_async_remote_copy(
+            src_ref=f_send.at[peer], dst_ref=f_recv.at[peer], send_sem=f_s.at[peer], recv_sem=f_r.at[peer],
+            device_id={"dp": peer}, device_id_type=MESH).wait_recv()
+    for r in range(n_dp):
+        block = slice(r * ocols, (r + 1) * ocols)
+        mine = hid32[0:seqs, block]
+        for q in range(1, n_tp):
+            mine = jnp.where(tp == q, hid32[q * seqs : (q + 1) * seqs, block], mine)
+        fin[:, block] = mine + f_recv[r].astype(F32)
+    resid = fin[...]
+    inverse = lax.rsqrt(jnp.sum(resid * resid, axis=1, keepdims=True) / width + F32(1e-06))
+    weighted = resid * gain[...]
+    peak = jnp.max(jnp.abs(weighted), axis=1, keepdims=True)
+    scale = (peak * inverse + F32(1e-06)) / F32(448.0)
+    scaled = (weighted * (inverse / scale)).astype(BF16)
+    for q in range(n_tp):
+        o_send[q, 0] = resid[:, q * owide : (q + 1) * owide].astype(BF16)
+        o_send[q, 1] = scaled[:, q * owide : (q + 1) * owide]
+    spread = jnp.where(lane_i == row_i + tp * seqs, jnp.broadcast_to(scale, lane_i.shape), F32(0.0))
+    c_send[...] = jnp.broadcast_to(jnp.sum(spread, axis=0, keepdims=True), c_send.shape)
+    for d in range(1, n_tp):
+        peer = lax.rem(tp + d, n_tp)
+        pending.append(send(c_send, c_recv.at[tp], c_s.at[peer], c_r.at[tp], {"tp": peer}))
+    pending += exchange(o_send, o_recv, o_s, o_r, lambda q: None)
+    scales = c_send[...]
+    for d in range(1, n_tp):
+        peer = lax.rem(tp + d, n_tp)
+        pltpu.make_async_remote_copy(
+            src_ref=c_send, dst_ref=c_recv.at[peer], send_sem=c_s.at[peer], recv_sem=c_r.at[peer],
+            device_id={"tp": peer}, device_id_type=MESH).wait_recv()
+        scales = scales + c_recv[peer]
+    scale_out[...] = scales
+    for part, out in ((0, resid_out), (1, scaled_out)):
+        for q in range(n_tp):
+            b_rows[q * seqs : (q + 1) * seqs, :] = o_recv[q, part].astype(F32)
+        out[...] = b_rows[...].astype(BF16)
+    for copy in pending:
+        copy.wait_send()
+
+
+def fused(n_dp, n_tp, hidden, w_qkv, w_out, norm_gain, kv_cache, lengths):
+    rows, width = hidden.shape
+    seqs, kvh, ctx, hd2 = kv_cache.shape
+    hd = hd2 // 2
+    depth, cols = w_qkv.shape
+    odepth, ocols = w_out.shape
+    heads = odepth * n_tp // hd
+    owide = width // n_tp
+    chips = n_dp // 2
+    vm = pltpu.VMEM
+    dma = pltpu.SemaphoreType.DMA
+    all_rows = seqs * heads
+    scratch = [
+        vm((2, chips, rows, depth), BF16), vm((depth, cols), BF16), vm((odepth, ocols), BF16),
+        vm(kv_cache.shape, BF16), vm((rows, width), BF16), vm((rows, width), F32),
+        vm((chips, rows, cols), BF16), vm((chips, rows, cols), BF16), vm((chips, rows, cols), F32),
+        vm((chips, rows, cols), BF16), vm((chips, rows, cols), BF16), vm((rows, cols), F32),
+        vm((n_tp, seqs, cols), BF16), vm((n_tp, seqs, cols), BF16),
+        vm((all_rows, hd), F32), vm((all_rows, hd), F32), vm((all_rows, hd), F32), vm((all_rows, hd), F32),
+        vm((all_rows, ctx), F32), vm((all_rows, hd), F32),
+        vm((n_tp, seqs, odepth), BF16), vm((n_tp, seqs, odepth), BF16), vm((rows, odepth), F32),
+        vm((2, chips, rows, odepth), BF16), vm((2, chips, rows, ocols), F32),
+        vm((n_tp, n_dp * seqs, ocols), F32), vm((n_tp, n_dp * seqs, ocols), BF16),
+        vm((n_tp, n_dp * seqs, ocols), BF16),
+        vm((n_dp, seqs, ocols), BF16), vm((n_dp, seqs, ocols), BF16),
+        vm((n_tp, 2, seqs, owide), BF16), vm((n_tp, 2, seqs, owide), BF16),
+        vm((8, hd), F32), vm((n_tp, 8, hd), F32), vm((seqs, width), F32),
+        dma((5,)), dma((n_dp,)), dma((n_dp,)), dma, dma, dma((chips,)), dma((chips,)),
+        dma((n_tp,)), dma((n_tp,)), dma((n_tp,)), dma((n_tp,)),
+        dma((chips,)), dma((2, chips)), dma((chips,)), dma((n_tp,)), dma((n_tp,)),
+        dma((n_dp,)), dma((n_dp,)), dma((n_tp,)), dma((n_tp,)), dma((n_tp,)), dma((n_tp,)),
+    ]
+    anywhere = pl.BlockSpec(memory_space=pl.ANY)
+    in_vmem = pl.BlockSpec(memory_space=pltpu.VMEM)
+    resid, scaled, scale = pl.pallas_call(
+        functools.partial(layer, n_dp, n_tp),
+        out_shape=(
+            jax.ShapeDtypeStruct((rows, owide), BF16),
+            jax.ShapeDtypeStruct((rows, owide), BF16),
+            jax.ShapeDtypeStruct((8, hd), F32),
+        ),
+        in_specs=[anywhere, anywhere, anywhere, in_vmem, anywhere, pl.BlockSpec(memory_space=pltpu.SMEM)],
+        out_specs=(in_vmem, in_vmem, in_vmem),
+        scratch_shapes=scratch,
+        compiler_params=pltpu.CompilerParams(
+            collective_id=0, has_side_effects=True, vmem_limit_bytes=66_000_000),
+    )(hidden, w_qkv, w_out, norm_gain.reshape(1, width), kv_cache, lengths)
+    return resid, scaled, scale[0, :rows]
+
+
 def solution(mesh):
     placed = (
         P("dp", None),
@@ -96,8 +425,25 @@
         P(("dp", "tp"), None, None, None),
         P(("dp", "tp")),
     )
+    n_dp, n_tp = mesh.shape["dp"], mesh.shape["tp"]
+
+    def body(hidden, w_qkv, w_out, norm_gain, kv_cache, lengths):
+        lanes = kv_cache.shape[3] // 2
+        fits = (
+            n_dp % 2 == 0
+            and kv_cache.shape[2] == lanes
+            and w_qkv.shape[1] % lanes == 0
+            and w_out.shape[0] % lanes == 0
+            and w_out.shape[1] % lanes == 0
+            and hidden.shape[0] <= lanes
+            and hidden.shape[1] // n_tp == w_out.shape[0]
+        )
+        if fits:
+            return fused(n_dp, n_tp, hidden, w_qkv, w_out, norm_gain, kv_cache, lengths)
+        return shards(hidden, w_qkv, w_out, norm_gain, kv_cache, lengths)
+
     return jax.shard_map(
-        shards,
+        body,
         mesh=mesh,
         in_specs=placed,
         out_specs=(P("dp", "tp"), P("dp", "tp"), P("dp")),

time: 242 us -> 68 us (0.28)
  waiting for transfers between devices: 180 us -> 0 us
  Pallas kernels: 0 us -> 62.8 us
  blocking collectives: 25.3 us -> 0 us
  between operations: 13.9 us -> 0.64 us
  matrix products: 12.4 us -> 0 us
  other arithmetic: 4.18 us -> 0 us
  starting transfers between devices: 3.72 us -> 0 us
  local copies, waits for them, and re-layouts: 1.69 us -> 4.26 us
    all_gather x2 -> x0, waiting for transfers between devices: 151 us -> none  [the longest x1 93.6 us: shards(): w_cols = lax.all_gather(w_qkv, 'dp', axis=0, tiled=True)]
    pallas_call x0 -> x1, Pallas kernels: none -> 62.8 us  [fused(): pl.pallas_call(functools.partial(layer, n_dp, n_tp), out_shape=(jax.Shape...]
    reduce_scatter x1 -> x0, waiting for transfers between devices: 22.7 us -> none  [shards(): lax.psum_scatter(terms.astype(jnp.bfloat16), 'tp', scatter_dimension=1, t...]
    dot_general x5 -> x0, matrix products: 12.4 us -> none  [the longest x1 5.7 us: shards(): jnp.dot(heads_part, lax.all_gather(w_out, 'dp', axis=1, tiled=True), pref...]
    pmax x1 -> x0, blocking collectives: 8.93 us -> none  [shards(): peak = lax.pmax(jnp.max(jnp.abs(weighted), axis=-1), 'tp')]
    psum x1 -> x0, blocking collectives: 8.87 us -> none  [shards(): squares = lax.psum(jnp.sum(resid_mine * resid_mine, axis=-1), 'tp')]
    all_to_all x1 -> x0, blocking collectives: 7.54 us -> none  [shards(): lax.all_to_all(attn, 'tp', split_axis=1, concat_axis=0, tiled=True)]
    all_to_all x1 -> x0, waiting for transfers between devices: 4.99 us -> none  [shards(): lax.all_to_all(qkv_part.astype(jnp.bfloat16), 'tp', split_axis=0, concat_...]
  transfers between devices with their start and end apart: 4 -> 0, of which waited for: 4 -> 0; matrix products, arithmetic and copies ran while one was open for 4% -> 0% of each run, Pallas kernels for 0% -> 0%
where the time goes in v1:
time: 68 us; the launch traced here: 67.7 us
  Pallas kernels  62.8 us (92%)
  local copies, waits for them, and re-layouts  4.26 us (6%)
    pallas_call x1, Pallas kernels, fused(): pl.pallas_call(functools.partial(layer, n_dp, n_tp), out_shape=(jax.Shape...  62.8 us
    unnamed x2, local copies, waits for them, and re-layouts  3.08 us

profile of v1, /device:TPU:0, one launch (start us, length us, event | category | flops | bytes accessed | tf_op | source)
XLA Modules:
  0.0 67.7 jit_solution(11881610685564080786)
XLA Ops:
  0.6 62.8 %shard_map.85 = (bf16[48,1024]{1,0:T(8,128)(2,1)}, bf16[48,1024]{1,0:T(8,128)(2,1)}, f32[8,128]{1,0:T(8,128)}) custom-call(bf16[48,4096]{1,0:T(8,128)(2,1)} %hidden.1, bf16[512,1152]{1,0:T(8,128)(2,1)} %w_qkv.1, bf16[1024,512]{1,0:T(8,128)(2,1)} %w_out.1, f32[1,4096]{1,0:T(1,128)} %bitcast.3, bf16[12,2,128,256]{3,2,1,0:T(8,128)(2,1)} %cache.1, s32[12]{0:T(128)} %lens.1), custom_call_target="tpu_custom_call" | custom-call | tf_op jit(solution)/shard_map/pallas_call | solution.py:403
  63.5 1.2 %slice_bitcast_fusion = f32[48]{0:T(128)} fusion(f32[8,128]{1,0:T(8,128)} %get-tuple-element.8), kind=kLoop, calls=%fused_computation | loop fusion | bytes 384 | tf_op jit(solution)/shard_map/squeeze | solution.py:416
  64.7 1.5 %copy.11 = bf16[48,1024]{1,0:T(8,128)(2,1)} copy(bf16[48,1024]{1,0:T(8,128)(2,1)} %get-tuple-element.12) | data formatting | bytes 196608
  66.2 1.5 %copy.12 = bf16[48,1024]{1,0:T(8,128)(2,1)} copy(bf16[48,1024]{1,0:T(8,128)(2,1)} %get-tuple-element.13) | data formatting | bytes 196608

commit v2 on v1

--- a/solution.py
+++ b/solution.py
@@ -109,12 +109,12 @@
     n_dp, n_tp,
     hidden, w_qkv, w_out, gain, cache, lens,
     resid_out, scaled_out, scale_out,
-    h_all, w1, w2, kv, hid, hid32, p_send, p_recv, r_acc, r_send, r_recv, mine32,
-    t1_send, t1_recv, q_rows, k_rows, v_rows, l_rows, s_rows, a_rows,
-    t2_send, t2_recv, b_rows, ag, mm, mq, t3_send, t3_recv, f_send, f_recv,
+    h_all, w1, w2, kv, hid, hid32, p_send, p_recv, r_acc, r_send, r_recv,
+    q_rows, k_rows, v_rows, l_rows, s_rows, a_rows,
+    t2_send, t2_recv, b_rows, ag, mm, f_send, f_recv,
     o_send, o_recv, c_send, c_recv, fin,
-    loc_sem, h_s, h_r, p_s, p_r, r_s, r_r, t1_s, t1_r, t2_s, t2_r,
-    g_s, g_r, x_s, t3_s, t3_r, f_s, f_r, o_s, o_r, c_s, c_r,
+    loc_sem, h_s, h_r, p_s, p_r, r_s, r_r, t2_s, t2_r,
+    g_s, g_r, x_s, f_s, f_r, o_s, o_r, c_s, c_r,
 ):
     dp = lax.axis_index("dp")
     tp = lax.axis_index("tp")
@@ -144,11 +144,13 @@
     load_w1.start()
 
     barrier = pltpu.get_barrier_semaphore()
-    for d in range(1, n_dp):
-        pl.semaphore_signal(barrier, inc=1, device_id={"dp": lax.rem(dp + d, n_dp)}, device_id_type=MESH)
-    for d in range(1, n_tp):
-        pl.semaphore_signal(barrier, inc=1, device_id={"tp": lax.rem(tp + d, n_tp)}, device_id_type=MESH)
-    pl.semaphore_wait(barrier, n_dp + n_tp - 2)
+    for d in range(n_dp):
+        for e in range(n_tp):
+            if d or e:
+                pl.semaphore_signal(
+                    barrier, inc=1, device_id_type=MESH,
+                    device_id={"dp": lax.rem(dp + d, n_dp), "tp": lax.rem(tp + e, n_tp)})
+    pl.semaphore_wait(barrier, n_dp * n_tp - 1)
 
     pending = []
     for d in range(1, n_dp):
@@ -199,18 +201,31 @@
     part = jnp.dot(h_all[core].reshape(n_chip * rows, depth), w1[...], preferred_element_type=F32)
     r_acc[...] = part.reshape(r_acc.shape)
     swap.wait_recv()
-    for d in range(1, n_chip):
+    order = sorted(range(n_chip), key=lambda d: -min(d, n_chip - d))
+    for d in order:
         to = lax.rem(chip + d, n_chip)
-        r_send[to] = (r_acc[to] + p_recv[to].astype(F32)).astype(BF16)
-        pending.append(send(r_send.at[to], r_recv.at[chip], r_s.at[to], r_r.at[chip], {"dp": to * 2 + core}))
-    total = r_acc[chip] + p_recv[chip].astype(F32)
-    for d in range(1, n_chip):
+        r_acc[to] = r_acc[to] + p_recv[to].astype(F32)
+        for q in range(n_tp):
+            r_send[to, q] = r_acc[to, q * seqs : (q + 1) * seqs, :].astype(BF16)
+        for e in reversed(range(n_tp)):
+            peer = lax.rem(tp + e, n_tp)
+            if d or e:
+                pending.append(send(
+                    r_send.at[to, peer], r_recv.at[chip, tp], r_s.at[to, peer], r_r.at[chip, tp],
+                    {"dp": to * 2 + core, "tp": peer}))
+            else:
+                keep = pltpu.make_async_copy(r_send.at[chip, tp], r_recv.at[chip, tp], loc_sem.at[0])
+                keep.start()
+    keep.wait()
+    for d in reversed(order):
         who = lax.rem(chip + d, n_chip)
-        pltpu.make_async_remote_copy(
-            src_ref=r_send.at[who], dst_ref=r_recv.at[who], send_sem=r_s.at[who], recv_sem=r_r.at[who],
-            device_id={"dp": who * 2 + core}, device_id_type=MESH).wait_recv()
-        total = total + r_recv[who].astype(F32)
-    mine32[...] = total
+        for e in range(n_tp):
+            peer = lax.rem(tp + e, n_tp)
+            if d or e:
+                pltpu.make_async_remote_copy(
+                    src_ref=r_send.at[who, peer], dst_ref=r_recv.at[who, peer],
+                    send_sem=r_s.at[who, peer], recv_sem=r_r.at[who, peer],
+                    device_id={"dp": who * 2 + core, "tp": peer}, device_id_type=MESH).wait_recv()
 
     def exchange(src, dst, s_sem, r_sem, fill):
         for q in range(n_tp):
@@ -229,13 +244,12 @@
                 device_id={"tp": peer}, device_id_type=MESH).wait_recv()
         return sent
 
-    def fill1(q):
-        t1_send[q] = mine32[q * seqs : (q + 1) * seqs, :].astype(BF16)
-
-    pending += exchange(t1_send, t1_recv, t1_s, t1_r, fill1)
-
     def head(h):
-        return t1_recv[h // per, :, (h % per) * hd : (h % per + 1) * hd].astype(F32)
+        at = slice((h % per) * hd, (h % per + 1) * hd)
+        total = r_recv[0, h // per, :, at].astype(F32)
+        for c in range(1, n_chip):
+            total = total + r_recv[c, h // per, :, at].astype(F32)
+        return total.astype(BF16).astype(F32)
 
     def turn(x):
         return (x * cosine + pltpu.roll(x, half, 1) * sine).astype(BF16).astype(F32)
@@ -299,42 +313,45 @@
         recv_g(core, who)
         pending.append(send(ag.at[core, who], ag.at[core, who], x_s.at[who], g_r.at[core, who], {"dp": partner}))
     load_w2.wait()
-    mm[core] = jnp.dot(ag[core].reshape(n_chip * rows, w_out.shape[0]), w2[...],
-                       preferred_element_type=F32).reshape(n_chip, rows, ocols)
+    def project(side):
+        mm[side] = jnp.dot(ag[side].reshape(n_chip * rows, w_out.shape[0]), w2[...],
+                           preferred_element_type=F32).reshape(n_chip, rows, ocols)
+        for d in order:
+            to = lax.rem(chip + d, n_chip)
+            for q in range(n_tp):
+                f_send[side, to, q] = mm[side, to, q * seqs : (q + 1) * seqs, :].astype(BF16)
+            for e in reversed(range(n_tp)):
+                peer = lax.rem(tp + e, n_tp)
+                if d or e or side is not core:
+                    pending.append(send(
+                        f_send.at[side, to, peer], f_recv.at[tp, dp], f_s.at[side, to, peer], f_r.at[tp, dp],
+                        {"dp": to * 2 + side, "tp": peer}))
+                else:
+                    pltpu.make_async_copy(f_send.at[side, to, peer], f_recv.at[tp, dp], loc_sem.at[0]).start()
+
+    project(core)
     for d in range(n_chip):
         recv_g(other, d)
-    mm[other] = jnp.dot(ag[other].reshape(n_chip * rows, w_out.shape[0]), w2[...],
-                        preferred_element_type=F32).reshape(n_chip, rows, ocols)
-
-    def fill3(q):
-        for r in range(n_dp):
-            mq[q, r * seqs : (r + 1) * seqs, :] = mm[r % 2, r // 2, q * seqs : (q + 1) * seqs, :]
-        t3_send[q] = mq[q].astype(BF16)
-
-    pending += exchange(t3_send, t3_recv, t3_s, t3_r, fill3)
-    total = t3_recv[0].astype(F32)
-    for q in range(1, n_tp):
-        total = total + t3_recv[q].astype(F32)
-    mq[0] = total
-    for r in range(n_dp):
-        f_send[r] = mq[0, r * seqs : (r + 1) * seqs, :].astype(BF16)
-    keep = pltpu.make_async_copy(f_send.at[dp], f_recv.at[dp], f_r.at[dp])
-    keep.start()
-    for d in range(1, n_dp):
-        peer = lax.rem(dp + d, n_dp)
-        pending.append(send(f_send.at[peer], f_recv.at[dp], f_s.at[peer], f_r.at[dp], {"dp": peer}))
-    keep.wait()
-    for d in range(1, n_dp):
-        peer = lax.rem(dp + d, n_dp)
-        pltpu.make_async_remote_copy(
-            src_ref=f_send.at[peer], dst_ref=f_recv.at[peer], send_sem=f_s.at[peer], recv_sem=f_r.at[peer],
-            device_id={"dp": peer}, device_id_type=MESH).wait_recv()
+    project(other)
+    pltpu.make_async_copy(f_send.at[core, chip, tp], f_recv.at[tp, dp], loc_sem.at[0]).wait()
+    for d in range(n_dp):
+        who = lax.rem(dp + d, n_dp)
+        for e in range(n_tp):
+            peer = lax.rem(tp + e, n_tp)
+            if d or e:
+                pltpu.make_async_remote_copy(
+                    src_ref=f_send.at[core, chip, peer], dst_ref=f_recv.at[peer, who],
+                    send_sem=f_s.at[core, chip, peer], recv_sem=f_r.at[peer, who],
+                    device_id={"dp": who, "tp": peer}, device_id_type=MESH).wait_recv()
     for r in range(n_dp):
         block = slice(r * ocols, (r + 1) * ocols)
         mine = hid32[0:seqs, block]
         for q in range(1, n_tp):
             mine = jnp.where(tp == q, hid32[q * seqs : (q + 1) * seqs, block], mine)
-        fin[:, block] = mine + f_recv[r].astype(F32)
+        total = f_recv[0, r].astype(F32)
+        for q in range(1, n_tp):
+            total = total + f_recv[q, r].astype(F32)
+        fin[:, block] = mine + total
     resid = fin[...]
     inverse = lax.rsqrt(jnp.sum(resid * resid, axis=1, keepdims=True) / width + F32(1e-06))
     weighted = resid * gain[...]
@@ -366,6 +383,12 @@
         copy.wait_send()
 
 
+def finish(resid, scaled, scale, resid_out, scaled_out, scale_out):
+    resid_out[...] = resid[...]
+    scaled_out[...] = scaled[...]
+    scale_out[...] = scale[0:1, : scale_out.shape[1]]
+
+
 def fused(n_dp, n_tp, hidden, w_qkv, w_out, norm_gain, kv_cache, lengths):
     rows, width = hidden.shape
     seqs, kvh, ctx, hd2 = kv_cache.shape
@@ -382,21 +405,18 @@
         vm((2, chips, rows, depth), BF16), vm((depth, cols), BF16), vm((odepth, ocols), BF16),
         vm(kv_cache.shape, BF16), vm((rows, width), BF16), vm((rows, width), F32),
         vm((chips, rows, cols), BF16), vm((chips, rows, cols), BF16), vm((chips, rows, cols), F32),
-        vm((chips, rows, cols), BF16), vm((chips, rows, cols), BF16), vm((rows, cols), F32),
-        vm((n_tp, seqs, cols), BF16), vm((n_tp, seqs, cols), BF16),
+        vm((chips, n_tp, seqs, cols), BF16), vm((chips, n_tp, seqs, cols), BF16),
         vm((all_rows, hd), F32), vm((all_rows, hd), F32), vm((all_rows, hd), F32), vm((all_rows, hd), F32),
         vm((all_rows, ctx), F32), vm((all_rows, hd), F32),
         vm((n_tp, seqs, odepth), BF16), vm((n_tp, seqs, odepth), BF16), vm((rows, odepth), F32),
         vm((2, chips, rows, odepth), BF16), vm((2, chips, rows, ocols), F32),
-        vm((n_tp, n_dp * seqs, ocols), F32), vm((n_tp, n_dp * seqs, ocols), BF16),
-        vm((n_tp, n_dp * seqs, ocols), BF16),
-        vm((n_dp, seqs, ocols), BF16), vm((n_dp, seqs, ocols), BF16),
+        vm((2, chips, n_tp, seqs, ocols), BF16), vm((n_tp, n_dp, seqs, ocols), BF16),
         vm((n_tp, 2, seqs, owide), BF16), vm((n_tp, 2, seqs, owide), BF16),
         vm((8, hd), F32), vm((n_tp, 8, hd), F32), vm((seqs, width), F32),
-        dma((5,)), dma((n_dp,)), dma((n_dp,)), dma, dma, dma((chips,)), dma((chips,)),
-        dma((n_tp,)), dma((n_tp,)), dma((n_tp,)), dma((n_tp,)),
-        dma((chips,)), dma((2, chips)), dma((chips,)), dma((n_tp,)), dma((n_tp,)),
-        dma((n_dp,)), dma((n_dp,)), dma((n_tp,)), dma((n_tp,)), dma((n_tp,)), dma((n_tp,)),
+        dma((5,)), dma((n_dp,)), dma((n_dp,)), dma, dma, dma((chips, n_tp)), dma((chips, n_tp)),
+        dma((n_tp,)), dma((n_tp,)),
+        dma((chips,)), dma((2, chips)), dma((chips,)),
+        dma((2, chips, n_tp)), dma((n_tp, n_dp)), dma((n_tp,)), dma((n_tp,)), dma((n_tp,)), dma((n_tp,)),
     ]
     anywhere = pl.BlockSpec(memory_space=pl.ANY)
     in_vmem = pl.BlockSpec(memory_space=pltpu.VMEM)
@@ -413,7 +433,17 @@
         compiler_params=pltpu.CompilerParams(
             collective_id=0, has_side_effects=True, vmem_limit_bytes=66_000_000),
     )(hidden, w_qkv, w_out, norm_gain.reshape(1, width), kv_cache, lengths)
-    return resid, scaled, scale[0, :rows]
+    resid, scaled, scale = pl.pallas_call(
+        finish,
+        out_shape=(
+            jax.ShapeDtypeStruct((rows, owide), BF16),
+            jax.ShapeDtypeStruct((rows, owide), BF16),
+            jax.ShapeDtypeStruct((1, rows), F32),
+        ),
+        in_specs=[in_vmem, in_vmem, in_vmem],
+        out_specs=(in_vmem, in_vmem, in_vmem),
+    )(resid, scaled, scale)
+    return resid, scaled, scale.reshape(rows)
 
 
 def solution(mesh):

time: 68 us -> 65 us (0.956)
  local copies, waits for them, and re-layouts: 4.26 us -> 0 us
  Pallas kernels: 62.8 us -> 64.1 us
    unnamed x2 -> x0, local copies, waits for them, and re-layouts: 3.08 us -> none
    pallas_call x0 -> x1, Pallas kernels: none -> 1.63 us  [fused(): pl.pallas_call(finish, out_shape=(jax.ShapeDtypeStruct((rows, owide), BF1...]
    squeeze x1 -> x0, local copies, waits for them, and re-layouts: 1.18 us -> none  [fused(): return (resid, scaled, scale[0, :rows])]
where the time goes in v2:
time: 65 us; the launch traced here: 64.7 us
  Pallas kernels  64.1 us (99%)
    pallas_call x1, Pallas kernels, fused(): pl.pallas_call(functools.partial(layer, n_dp, n_tp), out_shape=(jax.Shape...  62.4 us
    pallas_call x1, Pallas kernels, fused(): pl.pallas_call(finish, out_shape=(jax.ShapeDtypeStruct((rows, owide), BF1...  1.63 us

profile of v2, /device:TPU:0, one launch (start us, length us, event | category | flops | bytes accessed | tf_op | source)
XLA Modules:
  0.0 64.7 jit_solution(260601694871992458)
XLA Ops:
  0.6 62.4 %shard_map.85 = (bf16[48,1024]{1,0:T(8,128)(2,1)}, bf16[48,1024]{1,0:T(8,128)(2,1)}, f32[8,128]{1,0:T(8,128)}) custom-call(bf16[48,4096]{1,0:T(8,128)(2,1)} %hidden.1, bf16[512,1152]{1,0:T(8,128)(2,1)} %w_qkv.1, bf16[1024,512]{1,0:T(8,128)(2,1)} %w_out.1, f32[1,4096]{1,0:T(1,128)} %bitcast.2, bf16[12,2,128,256]{3,2,1,0:T(8,128)(2,1)} %cache.1, s32[12]{0:T(128)} %lens.1), custom_call_target="tpu_custom_call" | custom-call | tf_op jit(solution)/shard_map/pallas_call | solution.py:423
  63.1 1.6 %shard_map.86 = (bf16[48,1024]{1,0:T(8,128)(2,1)}, bf16[48,1024]{1,0:T(8,128)(2,1)}, f32[1,48]{1,0:T(1,128)}) custom-call(bf16[48,1024]{1,0:T(8,128)(2,1)} %get-tuple-element.9.resid, bf16[48,1024]{1,0:T(8,128)(2,1)} %get-tuple-element.10.scaled, f32[8,128]{1,0:T(8,128)} %get-tuple-element.11.scale), custom_call_target="tpu_custom_call" | custom-call | tf_op jit(solution)/shard_map/pallas_call | solution.py:436

commit v3 on v1

--- a/solution.py
+++ b/solution.py
@@ -299,31 +299,45 @@
         recv_g(core, who)
         pending.append(send(ag.at[core, who], ag.at[core, who], x_s.at[who], g_r.at[core, who], {"dp": partner}))
     load_w2.wait()
-    mm[core] = jnp.dot(ag[core].reshape(n_chip * rows, w_out.shape[0]), w2[...],
-                       preferred_element_type=F32).reshape(n_chip, rows, ocols)
+    def project(side):
+        mm[side] = jnp.dot(ag[side].reshape(n_chip * rows, w_out.shape[0]), w2[...],
+                           preferred_element_type=F32).reshape(n_chip, rows, ocols)
+        for q in range(n_tp):
+            for c in range(n_chip):
+                mq[q, side, c * seqs : (c + 1) * seqs, :] = mm[side, c, q * seqs : (q + 1) * seqs, :]
+            t3_send[q, side] = mq[q, side].astype(BF16)
+        for d in range(1, n_tp):
+            peer = lax.rem(tp + d, n_tp)
+            pending.append(send(
+                t3_send.at[peer, side], t3_recv.at[tp, side], t3_s.at[peer, side], t3_r.at[tp, side],
+                {"tp": peer}))
+
+    def scatter(side):
+        total = t3_send[tp, side].astype(F32)
+        for d in range(1, n_tp):
+            peer = lax.rem(tp + d, n_tp)
+            pltpu.make_async_remote_copy(
+                src_ref=t3_send.at[peer, side], dst_ref=t3_recv.at[peer, side],
+                send_sem=t3_s.at[peer, side], recv_sem=t3_r.at[peer, side],
+                device_id={"tp": peer}, device_id_type=MESH).wait_recv()
+            total = total + t3_recv[peer, side].astype(F32)
+        mq[0, side] = total
+        for c in range(n_chip):
+            f_send[2 * c + side] = mq[0, side, c * seqs : (c + 1) * seqs, :].astype(BF16)
+        for d in range(n_chip):
+            to = 2 * lax.rem(chip + d, n_chip) + side
+            if d or side is not core:
+                pending.append(send(f_send.at[to], f_recv.at[dp], f_s.at[to], f_r.at[dp], {"dp": to}))
+            else:
+                pltpu.make_async_copy(f_send.at[dp], f_recv.at[dp], loc_sem.at[0]).start()
+
+    project(core)
     for d in range(n_chip):
         recv_g(other, d)
-    mm[other] = jnp.dot(ag[other].reshape(n_chip * rows, w_out.shape[0]), w2[...],
-                        preferred_element_type=F32).reshape(n_chip, rows, ocols)
-
-    def fill3(q):
-        for r in range(n_dp):
-            mq[q, r * seqs : (r + 1) * seqs, :] = mm[r % 2, r // 2, q * seqs : (q + 1) * seqs, :]
-        t3_send[q] = mq[q].astype(BF16)
-
-    pending += exchange(t3_send, t3_recv, t3_s, t3_r, fill3)
-    total = t3_recv[0].astype(F32)
-    for q in range(1, n_tp):
-        total = total + t3_recv[q].astype(F32)
-    mq[0] = total
-    for r in range(n_dp):
-        f_send[r] = mq[0, r * seqs : (r + 1) * seqs, :].astype(BF16)
-    keep = pltpu.make_async_copy(f_send.at[dp], f_recv.at[dp], f_r.at[dp])
-    keep.start()
-    for d in range(1, n_dp):
-        peer = lax.rem(dp + d, n_dp)
-        pending.append(send(f_send.at[peer], f_recv.at[dp], f_s.at[peer], f_r.at[dp], {"dp": peer}))
-    keep.wait()
+    project(other)
+    scatter(core)
+    scatter(other)
+    pltpu.make_async_copy(f_send.at[dp], f_recv.at[dp], loc_sem.at[0]).wait()
     for d in range(1, n_dp):
         peer = lax.rem(dp + d, n_dp)
         pltpu.make_async_remote_copy(
@@ -366,6 +380,12 @@
         copy.wait_send()
 
 
+def finish(resid, scaled, scale, resid_out, scaled_out, scale_out):
+    resid_out[...] = resid[...]
+    scaled_out[...] = scaled[...]
+    scale_out[...] = scale[0:1, : scale_out.shape[1]]
+
+
 def fused(n_dp, n_tp, hidden, w_qkv, w_out, norm_gain, kv_cache, lengths):
     rows, width = hidden.shape
     seqs, kvh, ctx, hd2 = kv_cache.shape
@@ -388,14 +408,14 @@
         vm((all_rows, ctx), F32), vm((all_rows, hd), F32),
         vm((n_tp, seqs, odepth), BF16), vm((n_tp, seqs, odepth), BF16), vm((rows, odepth), F32),
         vm((2, chips, rows, odepth), BF16), vm((2, chips, rows, ocols), F32),
-        vm((n_tp, n_dp * seqs, ocols), F32), vm((n_tp, n_dp * seqs, ocols), BF16),
-        vm((n_tp, n_dp * seqs, ocols), BF16),
+        vm((n_tp, 2, chips * seqs, ocols), F32), vm((n_tp, 2, chips * seqs, ocols), BF16),
+        vm((n_tp, 2, chips * seqs, ocols), BF16),
         vm((n_dp, seqs, ocols), BF16), vm((n_dp, seqs, ocols), BF16),
         vm((n_tp, 2, seqs, owide), BF16), vm((n_tp, 2, seqs, owide), BF16),
         vm((8, hd), F32), vm((n_tp, 8, hd), F32), vm((seqs, width), F32),
         dma((5,)), dma((n_dp,)), dma((n_dp,)), dma, dma, dma((chips,)), dma((chips,)),
         dma((n_tp,)), dma((n_tp,)), dma((n_tp,)), dma((n_tp,)),
-        dma((chips,)), dma((2, chips)), dma((chips,)), dma((n_tp,)), dma((n_tp,)),
+        dma((chips,)), dma((2, chips)), dma((chips,)), dma((n_tp, 2)), dma((n_tp, 2)),
         dma((n_dp,)), dma((n_dp,)), dma((n_tp,)), dma((n_tp,)), dma((n_tp,)), dma((n_tp,)),
     ]
     anywhere = pl.BlockSpec(memory_space=pl.ANY)
@@ -413,7 +433,17 @@
         compiler_params=pltpu.CompilerParams(
             collective_id=0, has_side_effects=True, vmem_limit_bytes=66_000_000),
     )(hidden, w_qkv, w_out, norm_gain.reshape(1, width), kv_cache, lengths)
-    return resid, scaled, scale[0, :rows]
+    resid, scaled, scale = pl.pallas_call(
+        finish,
+        out_shape=(
+            jax.ShapeDtypeStruct((rows, owide), BF16),
+            jax.ShapeDtypeStruct((rows, owide), BF16),
+            jax.ShapeDtypeStruct((1, rows), F32),
+        ),
+        in_specs=[in_vmem, in_vmem, in_vmem],
+        out_specs=(in_vmem, in_vmem, in_vmem),
+    )(resid, scaled, scale)
+    return resid, scaled, scale.reshape(rows)
 
 
 def solution(mesh):

time: 68 us -> 63.2 us (0.929)
  local copies, waits for them, and re-layouts: 4.26 us -> 0 us
    unnamed x2 -> x0, local copies, waits for them, and re-layouts: 3.08 us -> none
    pallas_call x1, Pallas kernels: 62.8 us -> 60.6 us  [fused(): pl.pallas_call(functools.partial(layer, n_dp, n_tp), out_shape=(jax.Shape...]
    pallas_call x0 -> x1, Pallas kernels: none -> 1.63 us  [fused(): pl.pallas_call(finish, out_shape=(jax.ShapeDtypeStruct((rows, owide), BF1...]
    squeeze x1 -> x0, local copies, waits for them, and re-layouts: 1.18 us -> none  [fused(): return (resid, scaled, scale[0, :rows])]
where the time goes in v3:
time: 63.2 us; the launch traced here: 62.9 us
  Pallas kernels  62.3 us (99%)
  between operations  0.64 us (1%)
    pallas_call x1, Pallas kernels, fused(): pl.pallas_call(functools.partial(layer, n_dp, n_tp), out_shape=(jax.Shape...  60.6 us
    pallas_call x1, Pallas kernels, fused(): pl.pallas_call(finish, out_shape=(jax.ShapeDtypeStruct((rows, owide), BF1...  1.63 us

profile of v3, /device:TPU:0, one launch (start us, length us, event | category | flops | bytes accessed | tf_op | source)
XLA Modules:
  0.0 62.9 jit_solution(9268168678945535399)
XLA Ops:
  0.6 60.6 %shard_map.85 = (bf16[48,1024]{1,0:T(8,128)(2,1)}, bf16[48,1024]{1,0:T(8,128)(2,1)}, f32[8,128]{1,0:T(8,128)}) custom-call(bf16[48,4096]{1,0:T(8,128)(2,1)} %hidden.1, bf16[512,1152]{1,0:T(8,128)(2,1)} %w_qkv.1, bf16[1024,512]{1,0:T(8,128)(2,1)} %w_out.1, f32[1,4096]{1,0:T(1,128)} %bitcast.2, bf16[12,2,128,256]{3,2,1,0:T(8,128)(2,1)} %cache.1, s32[12]{0:T(128)} %lens.1), custom_call_target="tpu_custom_call" | custom-call | tf_op jit(solution)/shard_map/pallas_call | solution.py:423
  61.3 1.6 %shard_map.86 = (bf16[48,1024]{1,0:T(8,128)(2,1)}, bf16[48,1024]{1,0:T(8,128)(2,1)}, f32[1,48]{1,0:T(1,128)}) custom-call(bf16[48,1024]{1,0:T(8,128)(2,1)} %get-tuple-element.9.resid, bf16[48,1024]{1,0:T(8,128)(2,1)} %get-tuple-element.10.scaled, f32[8,128]{1,0:T(8,128)} %get-tuple-element.11.scale), custom_call_target="tpu_custom_call" | custom-call | tf_op jit(solution)/shard_map/pallas_call | solution.py:436

commit v4 on v3

--- a/solution.py
+++ b/solution.py
@@ -151,7 +151,7 @@
     pl.semaphore_wait(barrier, n_dp + n_tp - 2)
 
     pending = []
-    for d in range(1, n_dp):
+    for d in [*range(1, n_dp, 2), *range(2, n_dp, 2)]:
         peer = lax.rem(dp + d, n_dp)
         pending.append(send(
             hidden.at[:, pl.ds(pl.multiple_of(peer * depth, depth), depth)],
@@ -179,6 +179,12 @@
         l_rows[pl.ds(h, seqs, stride=heads), :] = live.astype(F32)
     load_hid.wait()
     hid32[...] = hid[...].astype(F32)
+    for r in range(n_dp):
+        block = slice(r * ocols, (r + 1) * ocols)
+        mine = hid32[0:seqs, block]
+        for q in range(1, n_tp):
+            mine = jnp.where(tp == q, hid32[q * seqs : (q + 1) * seqs, block], mine)
+        fin[:, block] = mine
 
     def recv_h(peer):
         pltpu.make_async_remote_copy(
@@ -345,10 +351,7 @@
             device_id={"dp": peer}, device_id_type=MESH).wait_recv()
     for r in range(n_dp):
         block = slice(r * ocols, (r + 1) * ocols)
-        mine = hid32[0:seqs, block]
-        for q in range(1, n_tp):
-            mine = jnp.where(tp == q, hid32[q * seqs : (q + 1) * seqs, block], mine)
-        fin[:, block] = mine + f_recv[r].astype(F32)
+        fin[:, block] = fin[:, block] + f_recv[r].astype(F32)
     resid = fin[...]
     inverse = lax.rsqrt(jnp.sum(resid * resid, axis=1, keepdims=True) / width + F32(1e-06))
     weighted = resid * gain[...]

time: 63.2 us -> 62.3 us (0.986)
  Pallas kernels: 62.3 us -> 61.5 us
    pallas_call x1, Pallas kernels: 60.6 us -> 59.8 us  [fused(): pl.pallas_call(functools.partial(layer, n_dp, n_tp), out_shape=(jax.Shape...]
where the time goes in v4:
time: 62.3 us; the launch traced here: 62.1 us
  Pallas kernels  61.5 us (99%)
  between operations  0.64 us (1%)
    pallas_call x1, Pallas kernels, fused(): pl.pallas_call(functools.partial(layer, n_dp, n_tp), out_shape=(jax.Shape...  59.8 us
    pallas_call x1, Pallas kernels, fused(): pl.pallas_call(finish, out_shape=(jax.ShapeDtypeStruct((rows, owide), BF1...  1.63 us

profile of v4, /device:TPU:0, one launch (start us, length us, event | category | flops | bytes accessed | tf_op | source)
XLA Modules:
  0.0 62.1 jit_solution(16555432539708509770)
XLA Ops:
  0.6 59.8 %shard_map.85 = (bf16[48,1024]{1,0:T(8,128)(2,1)}, bf16[48,1024]{1,0:T(8,128)(2,1)}, f32[8,128]{1,0:T(8,128)}) custom-call(bf16[48,4096]{1,0:T(8,128)(2,1)} %hidden.1, bf16[512,1152]{1,0:T(8,128)(2,1)} %w_qkv.1, bf16[1024,512]{1,0:T(8,128)(2,1)} %w_out.1, f32[1,4096]{1,0:T(1,128)} %bitcast.2, bf16[12,2,128,256]{3,2,1,0:T(8,128)(2,1)} %cache.1, s32[12]{0:T(128)} %lens.1), custom_call_target="tpu_custom_call" | custom-call | tf_op jit(solution)/shard_map/pallas_call | solution.py:426
  60.5 1.6 %shard_map.86 = (bf16[48,1024]{1,0:T(8,128)(2,1)}, bf16[48,1024]{1,0:T(8,128)(2,1)}, f32[1,48]{1,0:T(1,128)}) custom-call(bf16[48,1024]{1,0:T(8,128)(2,1)} %get-tuple-element.9.resid, bf16[48,1024]{1,0:T(8,128)(2,1)} %get-tuple-element.10.scaled, f32[8,128]{1,0:T(8,128)} %get-tuple-element.11.scale), custom_call_target="tpu_custom_call" | custom-call | tf_op jit(solution)/shard_map/pallas_call | solution.py:439

commit v5 on v4

--- a/solution.py
+++ b/solution.py
@@ -137,6 +137,8 @@
     per_out = w_out.shape[0] // hd
     width = hidden.shape[1]
 
+    load_hid = pltpu.make_async_copy(hidden, hid, loc_sem.at[4])
+    load_hid.start()
     own_h = pltpu.make_async_copy(
         hidden.at[:, pl.ds(pl.multiple_of(dp * depth, depth), depth)], h_all.at[core, chip], loc_sem.at[0])
     own_h.start()
@@ -150,18 +152,17 @@
         pl.semaphore_signal(barrier, inc=1, device_id={"tp": lax.rem(tp + d, n_tp)}, device_id_type=MESH)
     pl.semaphore_wait(barrier, n_dp + n_tp - 2)
 
+    load_hid.wait()
     pending = []
     for d in [*range(1, n_dp, 2), *range(2, n_dp, 2)]:
         peer = lax.rem(dp + d, n_dp)
         pending.append(send(
-            hidden.at[:, pl.ds(pl.multiple_of(peer * depth, depth), depth)],
+            hid.at[:, pl.ds(pl.multiple_of(peer * depth, depth), depth)],
             h_all.at[core, chip], h_s.at[peer], h_r.at[dp], {"dp": peer}))
     load_kv = pltpu.make_async_copy(cache, kv, loc_sem.at[2])
     load_kv.start()
     load_w2 = pltpu.make_async_copy(w_out, w2, loc_sem.at[3])
     load_w2.start()
-    load_hid = pltpu.make_async_copy(hidden, hid, loc_sem.at[4])
-    load_hid.start()
 
     row_i = lax.broadcasted_iota(jnp.int32, (seqs, hd), 0)
     lane_i = lax.broadcasted_iota(jnp.int32, (seqs, hd), 1)
@@ -177,7 +178,6 @@
     sine = jnp.where(low, -jnp.sin(angle), jnp.sin(angle))
     for h in range(heads):
         l_rows[pl.ds(h, seqs, stride=heads), :] = live.astype(F32)
-    load_hid.wait()
     hid32[...] = hid[...].astype(F32)
     for r in range(n_dp):
         block = slice(r * ocols, (r + 1) * ocols)

time: 62.3 us -> 62 us (level)
  no operation moved by 1% of the time
where the time goes in v5:
time: 62 us; the launch traced here: 61.8 us
  Pallas kernels  61.1 us (99%)
  between operations  0.64 us (1%)
    pallas_call x1, Pallas kernels, fused(): pl.pallas_call(functools.partial(layer, n_dp, n_tp), out_shape=(jax.Shape...  59.5 us
    pallas_call x1, Pallas kernels, fused(): pl.pallas_call(finish, out_shape=(jax.ShapeDtypeStruct((rows, owide), BF1...  1.63 us

profile of v5, /device:TPU:0, one launch (start us, length us, event | category | flops | bytes accessed | tf_op | source)
XLA Modules:
  0.0 61.8 jit_solution(16289963118117226068)
XLA Ops:
  0.6 59.5 %shard_map.85 = (bf16[48,1024]{1,0:T(8,128)(2,1)}, bf16[48,1024]{1,0:T(8,128)(2,1)}, f32[8,128]{1,0:T(8,128)}) custom-call(bf16[48,4096]{1,0:T(8,128)(2,1)} %hidden.1, bf16[512,1152]{1,0:T(8,128)(2,1)} %w_qkv.1, bf16[1024,512]{1,0:T(8,128)(2,1)} %w_out.1, f32[1,4096]{1,0:T(1,128)} %bitcast.2, bf16[12,2,128,256]{3,2,1,0:T(8,128)(2,1)} %cache.1, s32[12]{0:T(128)} %lens.1), custom_call_target="tpu_custom_call" | custom-call | tf_op jit(solution)/shard_map/pallas_call | solution.py:426
  60.1 1.6 %shard_map.86 = (bf16[48,1024]{1,0:T(8,128)(2,1)}, bf16[48,1024]{1,0:T(8,128)(2,1)}, f32[1,48]{1,0:T(1,128)}) custom-call(bf16[48,1024]{1,0:T(8,128)(2,1)} %get-tuple-element.9.resid, bf16[48,1024]{1,0:T(8,128)(2,1)} %get-tuple-element.10.scaled, f32[8,128]{1,0:T(8,128)} %get-tuple-element.11.scale), custom_call_target="tpu_custom_call" | custom-call | tf_op jit(solution)/shard_map/pallas_call | solution.py:439
